TPU v7x, 32 devices: a whole 2x2x4 slice. The times are simulated.
32 devices in a mesh: dp: 16 (over z, y, x), seq: 2 (over core).
Axes of the slice: x: 2, y: 2, z: 4, core: 2. Of those that a mesh axis runs over, the one named last changes fastest.
Arguments:
- chains_in: bfloat16 [128, 160, 768], P(('dp', 'seq')), may hold values from -6 to 6
- lengths: int32 [128], P(('dp', 'seq')), may hold values from 95 to 160
- d_out: bfloat16 [128, 160, 768], P(('dp', 'seq')), may hold values from -6 to 6
- w_query: bfloat16 [768, 768], replicated, may hold values from -0.21875 to 0.21875
- b_query: float32 [768], replicated, may hold values from -3 to 3
- w_key: bfloat16 [768, 768], replicated, may hold values from -0.21875 to 0.21875
- w_value: bfloat16 [768, 768], replicated, may hold values from -0.21875 to 0.21875
- b_value: float32 [768], replicated, may hold values from -3 to 3
- w_output: bfloat16 [768, 768], replicated, may hold values from -2.5 to 2.5
- b_output: float32 [768], replicated, may hold values from -3 to 3
- gain_one: float32 [768], replicated, may hold values from 0.25 to 1.75
- shift_one: float32 [768], replicated, may hold values from -2 to 2
- w_inner: bfloat16 [768, 3072], replicated, may hold values from -0.21875 to 0.21875
- b_inner: float32 [3072], replicated, may hold values from -3 to 3
- w_outer: bfloat16 [3072, 768], replicated, may hold values from -0.109375 to 0.109375
- b_outer: float32 [768], replicated, may hold values from -3 to 3
- gain_two: float32 [768], replicated, may hold values from 0.25 to 1.75
- shift_two: float32 [768], replicated, may hold values from -2 to 2
Outputs:
- layer_out: bfloat16 [128, 160, 768], P(('dp', 'seq'))
- d_x: float32 [128, 160, 768], P(('dp', 'seq'))
- d_w_query: float32 [768, 768], replicated
- d_b_query: float32 [768], replicated
- d_w_key: float32 [768, 768], replicated
- d_w_value: float32 [768, 768], replicated
- d_b_value: float32 [768], replicated
- d_w_output: float32 [768, 768], replicated
- d_b_output: float32 [768], replicated
- d_gain_one: float32 [768], replicated
- d_shift_one: float32 [768], replicated
- d_w_inner: float32 [768, 3072], replicated
- d_b_inner: float32 [3072], replicated
- d_w_outer: float32 [3072, 768], replicated
- d_b_outer: float32 [768], replicated
- d_gain_two: float32 [768], replicated
- d_shift_two: float32 [768], replicated
Inputs may be any that keep to these rules, and one draw needn't show every extreme that they name: `lengths`: every chain fills more than half of its 160 positions.
All inputs are finite; a program needn't handle non-finite values.
Results may differ from a plain program's by a relative error of at most 0.015.
Values may be sent and summed in bfloat16 or wider, within the bound.
No kernel may reach another device: no remote copies, remote signals or barrier semaphores. Data moves between devices by JAX's collectives and lax.ppermute only.
A program may use at most 256 MiB of HBM per device.

v0:
```python
import jax
import jax.numpy as jnp
from jax import lax
from jax.sharding import PartitionSpec as P

H = 12
EPS = 1e-12


def norm_forward(h, gain, shift):
    centre = h - jnp.mean(h, -1, keepdims=True)
    scale = lax.rsqrt(jnp.mean(centre * centre, -1, keepdims=True) + EPS)
    unit = centre * scale
    return (unit * gain + shift, unit, scale)


def norm_backward(grad, unit, scale, gain):
    d_gain = jnp.sum(grad * unit, 0)
    d_shift = jnp.sum(grad, 0)
    inner = grad * gain
    d_h = scale * (
        inner
        - jnp.mean(inner, -1, keepdims=True)
        - unit * jnp.mean(inner * unit, -1, keepdims=True)
    )
    return (d_h, d_gain, d_shift)


def over_rows(left, right):
    return lax.dot_general(
        left, right, (((0,), (0,)), ((), ())), preferred_element_type=jnp.float32
    )


def times_trans(left, weight):
    return lax.dot_general(
        left, weight, (((1,), (1,)), ((), ())), preferred_element_type=jnp.float32
    )


def attn_scores(query, keys, live_keys):
    seqs, count, width = query.shape
    total = keys.shape[1]
    size = width // H
    q_heads = query.reshape(seqs, count, H, size)
    k_heads = keys.reshape(seqs, total, H, size)
    scores = (
        jnp.einsum("bqhe,bkhe->bhqk", q_heads, k_heads, preferred_element_type=jnp.float32) * 0.125
    )
    return jnp.where(live_keys[:, None, None, :], scores, -1000000000.0)


def packed(grads, count):
    flat = jnp.concatenate([g.reshape(-1) for g in grads])
    extra = -flat.shape[0] % count
    return flat.reshape(count, -1)


def unpacked(flat, grads):
    flat = flat.reshape(-1)
    pieces = []
    start = 0
    for grad in grads:
        number = grad.size
        pieces.append(flat[start : start + number].reshape(grad.shape))
        start = start + number
    return tuple(pieces)


def body(
    chains_in,
    lengths,
    d_out,
    w_query,
    b_query,
    w_key,
    w_value,
    b_value,
    w_output,
    b_output,
    gain_one,
    shift_one,
    w_inner,
    b_inner,
    w_outer,
    b_outer,
    gain_two,
    shift_two,
):
    f32 = jnp.float32
    low_type = jnp.bfloat16
    seqs, length, width = chains_in.shape
    rows = seqs * length
    size = width // H
    parts = lax.axis_size("dp")
    count = lax.axis_size("dp") * lax.axis_size("seq")
    place = jnp.arange(length, dtype=jnp.int32)
    live_rows = place[None, :] < lengths[:, None]
    flat_x = chains_in.reshape(rows, width)
    query = (
        (jnp.dot(flat_x, w_query, preferred_element_type=f32) + b_query)
        .astype(low_type)
        .reshape(seqs, length, width)
    )
    keys = (
        jnp.dot(flat_x, w_key, preferred_element_type=f32)
        .astype(low_type)
        .reshape(seqs, length, width)
    )
    values = (
        (jnp.dot(flat_x, w_value, preferred_element_type=f32) + b_value)
        .astype(low_type)
        .reshape(seqs, length, width)
    )
    scores = attn_scores(query, keys, live_rows)
    top = jnp.max(scores, -1, keepdims=True)
    expo = jnp.exp(scores - top)
    summed = jnp.sum(expo, -1, keepdims=True)
    prob_b = (expo / summed).astype(low_type)
    lse = top + jnp.log(summed)
    v_heads = values.reshape(seqs, length, H, size)
    mixed = (
        jnp.einsum("bhqk,bkhe->bqhe", prob_b, v_heads, preferred_element_type=f32)
        .reshape(rows, width)
        .astype(low_type)
    )
    h_one = flat_x.astype(f32) + jnp.dot(mixed, w_output, preferred_element_type=f32) + b_output
    first, unit_one, scale_one = norm_forward(h_one, gain_one, shift_one)
    live_flat = live_rows.reshape(rows)
    fin = first.astype(low_type)
    pre = jnp.dot(fin, w_inner, preferred_element_type=f32) + b_inner
    hidden = jax.nn.gelu(pre, approximate=False).astype(low_type)
    ffn_home = (jnp.dot(hidden, w_outer, preferred_element_type=f32) + b_outer).astype(low_type)
    h_two = first + ffn_home.astype(f32)
    second, unit_two, scale_two = norm_forward(h_two, gain_two, shift_two)
    keep = live_flat[:, None].astype(f32)
    layer_out = (second * keep).astype(low_type).reshape(seqs, length, width)
    grad_out = d_out.reshape(rows, width).astype(f32) * keep
    d_h_two, d_gain_two, d_shift_two = norm_backward(grad_out, unit_two, scale_two, gain_two)
    d_ffn = d_h_two.astype(low_type)
    d_w_outer = over_rows(hidden, d_ffn)
    d_b_outer = jnp.sum(d_ffn.astype(f32), 0)
    d_hidden = times_trans(d_ffn, w_outer)
    gelu_pull = jax.vjp(lambda z: jax.nn.gelu(z, approximate=False), pre)[1]
    d_pre = gelu_pull(d_hidden)[0].astype(low_type)
    d_w_inner = over_rows(fin, d_pre)
    d_b_inner = jnp.sum(d_pre.astype(f32), 0)
    d_fin = times_trans(d_pre, w_inner).astype(low_type)
    d_home = d_fin
    d_first = d_h_two + d_home.astype(f32)
    ffn_grads = (d_w_inner, d_b_inner, d_w_outer, d_b_outer, d_gain_two, d_shift_two)
    d_h_one, d_gain_one, d_shift_one = norm_backward(d_first, unit_one, scale_one, gain_one)
    d_attn = d_h_one.astype(low_type)
    d_w_output = over_rows(mixed, d_attn)
    d_b_output = jnp.sum(d_attn.astype(f32), 0)
    d_mixed = times_trans(d_attn, w_output).astype(low_type).reshape(seqs, length, H, size)
    scores = attn_scores(query, keys, live_rows)
    prob = jnp.exp(scores - lse)
    prob_b = prob.astype(low_type)
    d_prob = jnp.einsum("bqhe,bkhe->bhqk", d_mixed, v_heads, preferred_element_type=f32)
    delta = jnp.sum(prob * d_prob, -1, keepdims=True)
    d_scores = (prob * (d_prob - delta)).astype(low_type)
    k_heads = keys.reshape(seqs, length, H, size)
    q_heads = query.reshape(seqs, length, H, size)
    d_query = (
        (jnp.einsum("bhqk,bkhe->bqhe", d_scores, k_heads, preferred_element_type=f32) * 0.125)
        .astype(low_type)
        .reshape(rows, width)
    )
    d_key = (
        (jnp.einsum("bhqk,bqhe->bkhe", d_scores, q_heads, preferred_element_type=f32) * 0.125)
        .astype(low_type)
        .reshape(rows, width)
    )
    d_value = (
        jnp.einsum("bhqk,bqhe->bkhe", prob_b, d_mixed, preferred_element_type=f32)
        .astype(low_type)
        .reshape(rows, width)
    )
    d_w_query = over_rows(flat_x, d_query)
    d_b_query = jnp.sum(d_query.astype(f32), 0)
    d_w_key = over_rows(flat_x, d_key)
    d_w_value = over_rows(flat_x, d_value)
    d_b_value = jnp.sum(d_value.astype(f32), 0)
    d_x = (
        d_h_one
        + times_trans(d_query, w_query)
        + times_trans(d_key, w_key)
        + times_trans(d_value, w_value)
    )
    d_x = d_x.reshape(seqs, length, width)
    attn_grads = (
        d_w_query,
        d_b_query,
        d_w_key,
        d_w_value,
        d_b_value,
        d_w_output,
        d_b_output,
        d_gain_one,
        d_shift_one,
    )
    local_grads = attn_grads + ffn_grads
    big = [g for g in local_grads if g.ndim == 2]
    small = [g for g in local_grads if g.ndim == 1]
    sums = lax.psum(jnp.concatenate(small), ("dp", "seq"))
    small_sums = unpacked(sums, small)
    big_sums = []
    for grad in big:
        part = lax.psum_scatter(
            grad.astype(low_type), ("dp", "seq"), scatter_dimension=0, tiled=True
        )
        big_sums.append(lax.all_gather(part, ("dp", "seq"), axis=0, tiled=True).astype(f32))
    every = []
    for grad in local_grads:
        every.append(big_sums.pop(0) if grad.ndim == 2 else small_sums[0])
        small_sums = small_sums if grad.ndim == 2 else small_sums[1:]
    return (
        layer_out,
        d_x,
        every[0],
        every[1],
        every[2],
        every[3],
        every[4],
        every[5],
        every[6],
        every[7],
        every[8],
        every[9],
        every[10],
        every[11],
        every[12],
        every[13],
        every[14],
    )


def solution(mesh):
    return jax.shard_map(
        body,
        mesh=mesh,
        in_specs=(
            P(("dp", "seq"), None, None),
            P(("dp", "seq")),
            P(("dp", "seq"), None, None),
            P(),
            P(),
            P(),
            P(),
            P(),
            P(),
            P(),
            P(),
            P(),
            P(),
            P(),
            P(),
            P(),
            P(),
            P(),
        ),
        out_specs=(
            P(("dp", "seq"), None, None),
            P(("dp", "seq"), None, None),
            P(),
            P(),
            P(),
            P(),
            P(),
            P(),
            P(),
            P(),
            P(),
            P(),
            P(),
            P(),
            P(),
            P(),
            P(),
        ),
        check_vma=False,
    )
```

profile of v0, /device:TPU:0, one launch (start us, length us, event | category | flops | bytes accessed | tf_op | source)
XLA Modules:
  0.0 1139.7 jit_solution(12008616428699110538)
XLA Ops:
  7.2 2.6 add_convert_fusion.3
  9.8 2.6 reshape.191
  12.5 4.6 copy.78
  17.1 2.5 add_convert_fusion.2
  19.6 2.6 reshape.192
  22.2 4.5 copy.76
  26.8 2.5 convolution_convert_fusion.8
  29.3 2.6 reshape.193
  31.9 3.5 copy.77
  35.4 3.6 fusion.12
  39.0 2.0 fusion.6
  42.2 2.5 fusion.20
  44.7 2.4 copy.80
  47.0 4.1 convert_element_type.174
  51.2 2.6 fusion.46
  53.8 1.3 copy-done.8
  55.6 23.9 %multiply_convert_fusion.1 = (bf16[640,3072]{1,0:T(8,128)(2,1)S(1)}, f32[640,3072]{1,0:T(8,128)}, f32[640,3072]{1,0:T(8,128)}) fusion(f32[3072]{0:T(1024)S(1)} %copy-done.22, bf16[768,3072]{1,0:T(8,128)(2,1)} %param.30, f32[640,768]{1,0:T(8,128)} %copy-done.8, f32[768]{0:T(1024)S(1)} %copy-done.26, f32[768]{0:T(1024)S(1)} %copy-done.19, ...), kind=kOutput, calls=%fused_computation.7 | convolution fusion | flops 3152117760 | bytes 26369024 | tf_op jit(solution)/shard_map/dot_general | solution.py:131
  79.5 7.2 fusion.47
  87.2 1.5 copy-done.5
  90.2 3.3 convert_reduce_fusion.3
  93.5 11.6 %convert_reduce_fusion = (f32[3072]{0:T(1024)S(1)}, bf16[640,3072]{1,0:T(8,128)(2,1)S(1)}) fusion(f32[640,3072]{1,0:T(8,128)} %get-tuple-element.64, bf16[3072,768]{1,0:T(8,128)(2,1)} %param.32, f32[640,768]{1,0:T(8,128)S(1)} %get-tuple-element.60, f32[640,3072]{1,0:T(8,128)} %get-tuple-element.80, f32[3072]{0:T(1024)S(1)} %copy-done.22), kind=kOutput, calls=%fused_computation.2 | convolution fusion | flops 3053810688 | bytes 26370048 | tf_op jit(solution)/shard_map/dot_general | solution.py:36
  105.2 3.8 multiply_reduce_fusion.2
  109.7 1.3 copy-done.6
  110.9 2.0 convolution_convert_fusion.7
  112.9 4.1 reshape.194
  117.0 4.6 copy.82
  121.6 7.5 multiply_reduce_fusion
  129.1 4.9 multiply_convert_fusion
  137.1 1.8 reshape.179
  138.9 3.6 fusion.26
  142.5 2.5 copy.100
  145.1 3.5 fusion.25
  148.6 1.2 copy.89
  149.8 1.8 reshape.180
  151.6 3.6 fusion.27
  155.2 2.5 copy.102
  157.8 5.5 convert_reduce_fusion.1
  164.5 2.0 reshape.181
  166.5 3.6 fusion.28
  170.1 2.5 copy.104
  172.8 3.3 convolution_convert_fusion.2
  176.2 9.1 convolution_convert_fusion.1
  185.3 8.8 convolution_convert_fusion
  194.3 49.8 %reduce-scatter.19.cloned.1.call-done = bf16[24,768]{1,0:T(8,128)(2,1)} async-done(((bf16[768,768]{1,0:T(8,128)(2,1)}), bf16[24,768]{1,0:T(8,128)(2,1)}) %reduce-scatter.19.cloned.1.call-update) | async-done | bytes 36880 | tf_op jit(solution)/shard_map/reduce_scatter | solution.py:210
  244.2 100.9 %reduce-scatter.21.cloned.1.call-done = bf16[24,768]{1,0:T(8,128)(2,1)} async-done(((bf16[768,768]{1,0:T(8,128)(2,1)}), bf16[24,768]{1,0:T(8,128)(2,1)}) %reduce-scatter.21.cloned.1.call-update) | async-done | bytes 36880 | tf_op jit(solution)/shard_map/reduce_scatter | solution.py:210
  345.1 100.4 %reduce-scatter.23.cloned.1.call-done = bf16[24,768]{1,0:T(8,128)(2,1)} async-done(((bf16[768,768]{1,0:T(8,128)(2,1)}), bf16[24,768]{1,0:T(8,128)(2,1)}) %reduce-scatter.23.cloned.1.call-update) | async-done | bytes 36880 | tf_op jit(solution)/shard_map/reduce_scatter | solution.py:210
  445.6 100.8 %reduce-scatter.13.cloned.1.call-done = bf16[24,768]{1,0:T(8,128)(2,1)} async-done(((bf16[768,768]{1,0:T(8,128)(2,1)}), bf16[24,768]{1,0:T(8,128)(2,1)}) %reduce-scatter.13.cloned.1.call-update) | async-done | bytes 36880 | tf_op jit(solution)/shard_map/reduce_scatter | solution.py:210
  546.4 111.9 %reduce-scatter.15.cloned.1.call-done = bf16[24,3072]{1,0:T(8,128)(2,1)} async-done(((bf16[768,3072]{1,0:T(8,128)(2,1)}), bf16[24,3072]{1,0:T(8,128)(2,1)}) %reduce-scatter.15.cloned.1.call-update) | async-done | bytes 147472 | tf_op jit(solution)/shard_map/reduce_scatter | solution.py:210
  658.4 112.9 %reduce-scatter.17.cloned.1.call-done = bf16[96,768]{1,0:T(8,128)(2,1)} async-done(((bf16[3072,768]{1,0:T(8,128)(2,1)}), bf16[96,768]{1,0:T(8,128)(2,1)}) %reduce-scatter.17.cloned.1.call-update) | async-done | bytes 147472 | tf_op jit(solution)/shard_map/reduce_scatter | solution.py:210
  771.5 40.6 %psum.7 = f32[9216]{0:T(1024)S(1)} all-reduce(f32[9216]{0:T(1024)S(1)} %constant_dynamic-update-slice_fusion), channel_id=1, replica_groups=mesh['dp'=16,'seq'=2] {'dp','seq'}, use_global_device_ids=true, to_apply=%region_21.22 | all-reduce | flops 9216 | bytes 73728 | tf_op jit(solution)/shard_map/psum | solution.py:206
  813.4 2.7 fusion.49
  817.7 2.3 add_add_fusion
  820.0 7.2 all-gather.7.cloned.1.call-done
  827.3 2.8 convert_element_type.202
  830.1 53.1 %all-gather.9.cloned.1.call-done = bf16[768,768]{1,0:T(8,128)(2,1)} async-done(((bf16[24,768]{1,0:T(8,128)(2,1)}), bf16[768,768]{1,0:T(8,128)(2,1)}) %all-gather.9.cloned.1.call-update) | async-done | bytes 1179664 | tf_op jit(solution)/shard_map/all_gather | solution.py:213
  883.2 2.8 convert_element_type.210
  886.0 53.1 %all-gather.11.cloned.1.call-done = bf16[768,768]{1,0:T(8,128)(2,1)} async-done(((bf16[24,768]{1,0:T(8,128)(2,1)}), bf16[768,768]{1,0:T(8,128)(2,1)}) %all-gather.11.cloned.1.call-update) | async-done | bytes 1179664 | tf_op jit(solution)/shard_map/all_gather | solution.py:213
  939.1 2.8 convert_element_type.213
  941.9 52.9 %all-gather.13.cloned.1.call-done = bf16[768,768]{1,0:T(8,128)(2,1)} async-done(((bf16[24,768]{1,0:T(8,128)(2,1)}), bf16[768,768]{1,0:T(8,128)(2,1)}) %all-gather.13.cloned.1.call-update) | async-done | bytes 1179664 | tf_op jit(solution)/shard_map/all_gather | solution.py:213
  994.8 2.8 convert_element_type.215
  997.7 62.7 %all-gather.15.cloned.1.call-done = bf16[768,3072]{1,0:T(8,128)(2,1)} async-done(((bf16[24,3072]{1,0:T(8,128)(2,1)}), bf16[768,3072]{1,0:T(8,128)(2,1)}) %all-gather.15.cloned.1.call-update) | async-done | bytes 4718608 | tf_op jit(solution)/shard_map/all_gather | solution.py:213
  1060.4 7.4 convert_element_type.217
  1067.7 57.9 %all-gather.17.cloned.1.call-done = bf16[3072,768]{1,0:T(8,128)(2,1)} async-done(((bf16[96,768]{1,0:T(8,128)(2,1)}), bf16[3072,768]{1,0:T(8,128)(2,1)}) %all-gather.17.cloned.1.call-update) | async-done | bytes 4718608 | tf_op jit(solution)/shard_map/all_gather | solution.py:213
  1125.6 6.8 convert_element_type.219
  (118 shorter events, 12.3 us)
Async XLA Ops:
  7.2 43.9 %copy-start = (bf16[768,768]{1,0:T(8,128)(2,1)S(1)}, bf16[768,768]{1,0:T(8,128)(2,1)}, u32[]{:S(2)}) copy-start(bf16[768,768]{1,0:T(8,128)(2,1)} %param.26) | copy-start | bytes 3538948
  7.2 236.9 %reduce-scatter.19.cloned.1.call-start = ((), (), s32[]{:S(2)}) async-start(), calls=%async_computation.15 | async-start | bytes 1216512 | tf_op jit(solution)/shard_map/reduce_scatter | solution.py:210
  12.5 4.6 copy-start.20
  12.5 4.6 copy-start.23
  39.0 3.2 copy-start.1
  39.0 3.2 copy-start.11
  44.6 6.5 copy-start.24
  51.1 4.4 copy-start.19
  51.1 4.4 copy-start.22
  51.1 4.4 copy-start.26
  53.8 1.3 copy-start.8
  55.5 24.0 %copy-start.9 = (f32[640,768]{1,0:T(8,128)S(1)}, f32[640,768]{1,0:T(8,128)}, u32[]{:S(2)}) copy-start(f32[640,768]{1,0:T(8,128)} %copy-done.8) | copy-start | bytes 5898244
  55.5 24.0 %copy-start.25 = (f32[768]{0:T(1024)S(1)}, f32[768]{0:T(1024)}, u32[]{:S(2)}) copy-start(f32[768]{0:T(1024)} %param.33) | copy-start | bytes 9220
  79.5 7.2 copy-start.27
  79.5 7.6 copy-start.17
  86.7 3.3 copy-start.3
  86.7 1.9 copy-start.5
  87.1 3.0 copy-start.18
  90.2 15.0 %slice-start = ((s8[4718592]{0:T(1024)(128)(4,1)}), s8[4194304]{0:T(1024)(128)(4,1)S(1)}, s32[]{:S(2)}) async-start(s8[4718592]{0:T(1024)(128)(4,1)} %bitcast.81), calls=%async_computation.18 | async-start | bytes 8388608
  93.5 11.7 %copy-start.14 = (f32[640,768]{1,0:T(8,128)}, f32[640,768]{1,0:T(8,128)S(1)}, u32[]{:S(2)}) copy-start(f32[640,768]{1,0:T(8,128)S(1)} %get-tuple-element.60) | copy-start | bytes 5898244
  93.5 11.7 %copy-start.10 = (f32[640,768]{1,0:T(8,128)S(1)}, f32[640,768]{1,0:T(8,128)}, u32[]{:S(2)}) copy-start(f32[640,768]{1,0:T(8,128)} %copy-done.8) | copy-start | bytes 5898244
  93.5 11.7 %slice-start.1 = ((s8[4718592]{0:T(1024)(128)(4,1)}), s8[524288]{0:T(1024)(128)(4,1)S(1)}, s32[]{:S(2)}) async-start(s8[4718592]{0:T(1024)(128)(4,1)} %bitcast.81), calls=%async_computation.19 | async-start | bytes 1048576
  105.1 3.9 copy-start.28
  109.7 1.3 copy-start.6
  134.0 1.9 copy-start.2
  142.5 2.6 copy-start.4
  145.0 200.0 %reduce-scatter.21.cloned.1.call-start = ((), (), s32[]{:S(2)}) async-start(), calls=%async_computation.16 | async-start | bytes 1216512 | tf_op jit(solution)/shard_map/reduce_scatter | solution.py:210
  155.2 2.6 copy-start.12
  157.7 287.8 %reduce-scatter.23.cloned.1.call-start = ((), (), s32[]{:S(2)}) async-start(), calls=%async_computation.17 | async-start | bytes 1216512 | tf_op jit(solution)/shard_map/reduce_scatter | solution.py:210
  170.1 2.6 copy-start.7
  172.7 373.6 %reduce-scatter.13.cloned.1.call-start = ((), (), s32[]{:S(2)}) async-start(), calls=%async_computation.9 | async-start | bytes 1216512 | tf_op jit(solution)/shard_map/reduce_scatter | solution.py:210
  176.1 482.2 %reduce-scatter.15.cloned.1.call-start = ((), (), s32[]{:S(2)}) async-start(), calls=%async_computation.11 | async-start | bytes 4866048 | tf_op jit(solution)/shard_map/reduce_scatter | solution.py:210
  185.3 585.9 %reduce-scatter.17.cloned.1.call-start = ((), (), s32[]{:S(2)}) async-start(), calls=%async_computation.13 | async-start | bytes 4866048 | tf_op jit(solution)/shard_map/reduce_scatter | solution.py:210
  194.2 633.1 %all-gather.7.cloned.1.call-start = ((), (), s32[]{:S(2)}) async-start(), calls=%async_computation.6 | async-start | bytes 1216512 | tf_op jit(solution)/shard_map/all_gather | solution.py:213
  244.1 639.1 %all-gather.9.cloned.1.call-start = ((), (), s32[]{:S(2)}) async-start(), calls=%async_computation.7 | async-start | bytes 1216512 | tf_op jit(solution)/shard_map/all_gather | solution.py:213
  345.0 594.0 %all-gather.11.cloned.1.call-start = ((), (), s32[]{:S(2)}) async-start(), calls=%async_computation.8 | async-start | bytes 1216512 | tf_op jit(solution)/shard_map/all_gather | solution.py:213
  445.5 549.3 %all-gather.13.cloned.1.call-start = ((), (), s32[]{:S(2)}) async-start(), calls=%async_computation.10 | async-start | bytes 1216512 | tf_op jit(solution)/shard_map/all_gather | solution.py:213
  546.3 514.0 %all-gather.15.cloned.1.call-start = ((), (), s32[]{:S(2)}) async-start(), calls=%async_computation.12 | async-start | bytes 4866048 | tf_op jit(solution)/shard_map/all_gather | solution.py:213
  658.3 467.3 %all-gather.17.cloned.1.call-start = ((), (), s32[]{:S(2)}) async-start(), calls=%async_computation.14 | async-start | bytes 4866048 | tf_op jit(solution)/shard_map/all_gather | solution.py:213
  812.7 3.4 copy-start.16
  812.7 3.4 copy-start.21
  816.1 1.2 copy-start.13
  816.1 1.6 copy-start.15
Sparse Core Ops, SparseCore 0:
  145.2 98.8 reduce-scatter.18
  249.7 95.2 reduce-scatter.20
  350.1 95.3 reduce-scatter.22
  451.0 95.2 reduce-scatter.12
  552.2 106.0 reduce-scatter.14
  665.1 106.0 reduce-scatter.16
  774.1 53.1 all-gather.6
  830.2 52.9 all-gather.8
  886.1 52.9 all-gather.10
  941.8 52.9 all-gather.12
  997.7 62.5 all-gather.14
  1063.1 62.4 all-gather.16
where the time goes:
time: 1150 us; the launch traced here: 1140 us
  waiting for transfers between devices  864 us (75%)
  matrix products  120 us (10%)
  local copies, waits for them, and re-layouts  60.8 us (5%)
  blocking collectives  40.6 us (4%)
  other arithmetic  38.7 us (3%)
  between operations  15.3 us (1%)
    reduce_scatter x6, waiting for transfers between devices, body(): lax.psum_scatter(grad.astype(low_type), ('dp', 'seq'), scatter_dimension=...  577 us
    all_gather x6, waiting for transfers between devices, body(): lax.all_gather(part, ('dp', 'seq'), axis=0, tiled=True).astype(f32)  287 us
    psum x1, blocking collectives, body(): sums = lax.psum(jnp.concatenate(small), ('dp', 'seq'))  40.6 us
    dot_general x6, matrix products, over_rows(): lax.dot_general(left, right, (((0,), (0,)), ((), ())), preferred_element_...  32.1 us
    convert_element_type x6, other arithmetic, body(): lax.all_gather(part, ('dp', 'seq'), axis=0, tiled=True).astype(f32)  25.6 us
    dot_general x1, matrix products, body(): pre = jnp.dot(fin, w_inner, preferred_element_type=f32) + b_inner  23.9 us
    dot_general x6, matrix products, times_trans(): lax.dot_general(left, weight, (((1,), (1,)), ((), ())), preferred_element...  23.5 us
  transfers between devices with their start and end apart: 12, of which 12 were waited for; matrix products, arithmetic and copies ran while one was open for 7% of the time, Pallas kernels for 0%

commit v1 on v0

--- a/solution.py
+++ b/solution.py
@@ -1,3 +1,4 @@
+import functools
 import jax
 import jax.numpy as jnp
 from jax import lax
@@ -5,6 +6,13 @@
 
 H = 12
 EPS = 1e-12
+
+
+def push_the_sector(a0, named_axis):
+    return lax.all_gather(a0, named_axis).sum(axis=0)
+
+
+guide_the_notes = functools.partial(push_the_sector, named_axis=("dp", "seq"))
 
 
 def norm_forward(h, gain, shift):
@@ -203,7 +211,7 @@
     local_grads = attn_grads + ffn_grads
     big = [g for g in local_grads if g.ndim == 2]
     small = [g for g in local_grads if g.ndim == 1]
-    sums = lax.psum(jnp.concatenate(small), ("dp", "seq"))
+    sums = guide_the_notes(jnp.concatenate(small))
     small_sums = unpacked(sums, small)
     big_sums = []
     for grad in big:

time: 1150 us -> 1210 us (1.052)
  waiting for transfers between devices: 864 us -> 958 us
  blocking collectives: 40.6 us -> 0 us
    all_gather x0 -> x1, waiting for transfers between devices: none -> 50 us  [push_the_sector(): return lax.all_gather(a0, named_axis).sum(axis=0)]
    all_gather x6, waiting for transfers between devices: 287 us -> 333 us  [body(): lax.all_gather(part, ('dp', 'seq'), axis=0, tiled=True).astype(f32)]
    psum x1 -> x0, blocking collectives: 40.6 us -> none  [body(): sums = lax.psum(jnp.concatenate(small), ('dp', 'seq'))]
  transfers between devices with their start and end apart: 12 -> 13, of which waited for: 12 -> 13; matrix products, arithmetic and copies ran while one was open for 7% -> 6% of each run, Pallas kernels for 0% -> 0%
where the time goes in v1:
time: 1210 us; the launch traced here: 1200 us
  waiting for transfers between devices  958 us (79%)
  matrix products  120 us (10%)
  local copies, waits for them, and re-layouts  62.8 us (5%)
  other arithmetic  38.8 us (3%)
  between operations  15 us (1%)
    reduce_scatter x6, waiting for transfers between devices, body(): lax.psum_scatter(grad.astype(low_type), ('dp', 'seq'), scatter_dimension=...  575 us
    all_gather x6, waiting for transfers between devices, body(): lax.all_gather(part, ('dp', 'seq'), axis=0, tiled=True).astype(f32)  333 us
    all_gather x1, waiting for transfers between devices, push_the_sector(): return lax.all_gather(a0, named_axis).sum(axis=0)  50 us
    dot_general x6, matrix products, over_rows(): lax.dot_general(left, right, (((0,), (0,)), ((), ())), preferred_element_...  32.1 us
    convert_element_type x6, other arithmetic, body(): lax.all_gather(part, ('dp', 'seq'), axis=0, tiled=True).astype(f32)  25.6 us
  transfers between devices with their start and end apart: 13, of which 13 were waited for; matrix products, arithmetic and copies ran while one was open for 6% of the time, Pallas kernels for 0%

profile of v1, /device:TPU:0, one launch (start us, length us, event | category | flops | bytes accessed | tf_op | source)
XLA Modules:
  0.0 1195.8 jit_solution(10338582150074028869)
XLA Ops:
  7.2 2.6 add_convert_fusion.3
  9.8 2.6 reshape.192
  12.5 4.6 copy.101
  17.1 2.5 add_convert_fusion.2
  19.6 2.6 reshape.193
  22.2 4.5 copy.99
  26.8 2.5 convolution_convert_fusion.8
  29.3 2.6 reshape.194
  31.9 3.5 copy.100
  35.4 3.6 fusion.12
  39.0 2.0 fusion.6
  42.2 2.5 fusion.20
  44.7 2.4 copy.103
  47.0 4.1 convert_element_type.174
  51.1 2.6 fusion.46
  53.8 1.3 copy-done.8
  55.5 23.9 %multiply_convert_fusion.1 = (bf16[640,3072]{1,0:T(8,128)(2,1)S(1)}, f32[640,3072]{1,0:T(8,128)}, f32[640,3072]{1,0:T(8,128)}) fusion(f32[3072]{0:T(1024)S(1)} %copy-done.23, bf16[768,3072]{1,0:T(8,128)(2,1)} %param.30, f32[640,768]{1,0:T(8,128)} %copy-done.8, f32[768]{0:T(1024)S(1)} %copy-done.27, f32[768]{0:T(1024)S(1)} %copy-done.20, ...), kind=kOutput, calls=%fused_computation.7 | convolution fusion | flops 3152117760 | bytes 26369024 | tf_op jit(solution)/shard_map/dot_general | solution.py:139
  79.5 7.2 fusion.47
  87.1 1.5 copy-done.5
  90.2 3.3 convert_reduce_fusion.3
  93.5 11.6 convert_reduce_fusion
  105.2 3.8 multiply_reduce_fusion.2
  109.7 1.3 copy-done.6
  110.9 2.0 convolution_convert_fusion.7
  112.9 4.1 reshape.195
  117.0 4.5 copy.105
  121.5 7.5 multiply_reduce_fusion
  129.0 4.9 multiply_convert_fusion
  137.1 1.8 reshape.179
  138.8 3.6 fusion.26
  142.4 2.5 copy.123
  145.1 3.5 fusion.25
  149.8 1.8 reshape.180
  151.5 3.6 fusion.27
  155.1 2.5 copy.125
  157.7 5.5 convert_reduce_fusion.1
  164.5 2.0 reshape.181
  166.5 3.6 fusion.28
  170.1 2.6 copy.127
  172.7 3.3 convolution_convert_fusion.2
  176.1 9.1 convolution_convert_fusion.1
  185.3 8.8 convolution_convert_fusion
  195.1 48.9 %reduce-scatter.19.cloned.1.call-done = bf16[24,768]{1,0:T(8,128)(2,1)} async-done(((bf16[768,768]{1,0:T(8,128)(2,1)}), bf16[24,768]{1,0:T(8,128)(2,1)}) %reduce-scatter.19.cloned.1.call-update) | async-done | bytes 36880 | tf_op jit(solution)/shard_map/reduce_scatter | solution.py:218
  244.1 100.9 %reduce-scatter.21.cloned.1.call-done = bf16[24,768]{1,0:T(8,128)(2,1)} async-done(((bf16[768,768]{1,0:T(8,128)(2,1)}), bf16[24,768]{1,0:T(8,128)(2,1)}) %reduce-scatter.21.cloned.1.call-update) | async-done | bytes 36880 | tf_op jit(solution)/shard_map/reduce_scatter | solution.py:218
  345.1 100.4 %reduce-scatter.23.cloned.1.call-done = bf16[24,768]{1,0:T(8,128)(2,1)} async-done(((bf16[768,768]{1,0:T(8,128)(2,1)}), bf16[24,768]{1,0:T(8,128)(2,1)}) %reduce-scatter.23.cloned.1.call-update) | async-done | bytes 36880 | tf_op jit(solution)/shard_map/reduce_scatter | solution.py:218
  445.5 100.8 %reduce-scatter.13.cloned.1.call-done = bf16[24,768]{1,0:T(8,128)(2,1)} async-done(((bf16[768,768]{1,0:T(8,128)(2,1)}), bf16[24,768]{1,0:T(8,128)(2,1)}) %reduce-scatter.13.cloned.1.call-update) | async-done | bytes 36880 | tf_op jit(solution)/shard_map/reduce_scatter | solution.py:218
  546.3 111.8 %reduce-scatter.15.cloned.1.call-done = bf16[24,3072]{1,0:T(8,128)(2,1)} async-done(((bf16[768,3072]{1,0:T(8,128)(2,1)}), bf16[24,3072]{1,0:T(8,128)(2,1)}) %reduce-scatter.15.cloned.1.call-update) | async-done | bytes 147472 | tf_op jit(solution)/shard_map/reduce_scatter | solution.py:218
  658.5 112.7 %reduce-scatter.17.cloned.1.call-done = bf16[96,768]{1,0:T(8,128)(2,1)} async-done(((bf16[3072,768]{1,0:T(8,128)(2,1)}), bf16[96,768]{1,0:T(8,128)(2,1)}) %reduce-scatter.17.cloned.1.call-update) | async-done | bytes 147472 | tf_op jit(solution)/shard_map/reduce_scatter | solution.py:218
  771.2 2.7 fusion.49
  775.5 2.3 add_add_fusion
  777.8 50.0 %all-gather.21.cloned.1.call-done = f32[294912]{0:T(1024)} async-done(((f32[9216]{0:T(1024)}), f32[294912]{0:T(1024)}) %all-gather.21.cloned.1.call-update) | async-done | bytes 1179664 | tf_op jit(solution)/shard_map/all_gather | solution.py:12
  827.8 1.4 reshape.185
  830.6 53.1 %all-gather.9.cloned.1.call-done = bf16[768,768]{1,0:T(8,128)(2,1)} async-done(((bf16[24,768]{1,0:T(8,128)(2,1)}), bf16[768,768]{1,0:T(8,128)(2,1)}) %all-gather.9.cloned.1.call-update) | async-done | bytes 1179664 | tf_op jit(solution)/shard_map/all_gather | solution.py:221
  883.7 2.8 convert_element_type.202
  886.6 53.1 %all-gather.11.cloned.1.call-done = bf16[768,768]{1,0:T(8,128)(2,1)} async-done(((bf16[24,768]{1,0:T(8,128)(2,1)}), bf16[768,768]{1,0:T(8,128)(2,1)}) %all-gather.11.cloned.1.call-update) | async-done | bytes 1179664 | tf_op jit(solution)/shard_map/all_gather | solution.py:221
  939.6 2.8 convert_element_type.210
  942.5 52.9 %all-gather.13.cloned.1.call-done = bf16[768,768]{1,0:T(8,128)(2,1)} async-done(((bf16[24,768]{1,0:T(8,128)(2,1)}), bf16[768,768]{1,0:T(8,128)(2,1)}) %all-gather.13.cloned.1.call-update) | async-done | bytes 1179664 | tf_op jit(solution)/shard_map/all_gather | solution.py:221
  995.4 2.8 convert_element_type.213
  998.2 53.1 %all-gather.15.cloned.1.call-done = bf16[768,768]{1,0:T(8,128)(2,1)} async-done(((bf16[24,768]{1,0:T(8,128)(2,1)}), bf16[768,768]{1,0:T(8,128)(2,1)}) %all-gather.15.cloned.1.call-update) | async-done | bytes 1179664 | tf_op jit(solution)/shard_map/all_gather | solution.py:221
  1051.3 2.8 convert_element_type.215
  1054.1 62.5 %all-gather.17.cloned.1.call-done = bf16[768,3072]{1,0:T(8,128)(2,1)} async-done(((bf16[24,3072]{1,0:T(8,128)(2,1)}), bf16[768,3072]{1,0:T(8,128)(2,1)}) %all-gather.17.cloned.1.call-update) | async-done | bytes 4718608 | tf_op jit(solution)/shard_map/all_gather | solution.py:221
  1116.7 7.4 convert_element_type.217
  1124.0 58.0 %all-gather.19.cloned.1.call-done = bf16[3072,768]{1,0:T(8,128)(2,1)} async-done(((bf16[96,768]{1,0:T(8,128)(2,1)}), bf16[3072,768]{1,0:T(8,128)(2,1)}) %all-gather.19.cloned.1.call-update) | async-done | bytes 4718608 | tf_op jit(solution)/shard_map/all_gather | solution.py:221
  1182.0 6.8 convert_element_type.219
  (124 shorter events, 14.5 us)
Async XLA Ops:
  7.2 43.9 %copy-start = (bf16[768,768]{1,0:T(8,128)(2,1)S(1)}, bf16[768,768]{1,0:T(8,128)(2,1)}, u32[]{:S(2)}) copy-start(bf16[768,768]{1,0:T(8,128)(2,1)} %param.26) | copy-start | bytes 3538948
  7.2 236.8 %reduce-scatter.19.cloned.1.call-start = ((), (), s32[]{:S(2)}) async-start(), calls=%async_computation.16 | async-start | bytes 1216512 | tf_op jit(solution)/shard_map/reduce_scatter | solution.py:218
  12.5 4.6 copy-start.21
  12.5 4.6 copy-start.24
  39.0 3.2 copy-start.1
  39.0 3.2 copy-start.11
  44.6 6.5 copy-start.25
  51.1 4.4 copy-start.20
  51.1 4.4 copy-start.23
  51.1 4.4 copy-start.27
  53.8 1.3 copy-start.8
  55.5 24.0 %copy-start.9 = (f32[640,768]{1,0:T(8,128)S(1)}, f32[640,768]{1,0:T(8,128)}, u32[]{:S(2)}) copy-start(f32[640,768]{1,0:T(8,128)} %copy-done.8) | copy-start | bytes 5898244
  55.5 24.0 %copy-start.26 = (f32[768]{0:T(1024)S(1)}, f32[768]{0:T(1024)}, u32[]{:S(2)}) copy-start(f32[768]{0:T(1024)} %param.33) | copy-start | bytes 9220
  79.5 7.2 copy-start.28
  79.5 7.6 copy-start.18
  86.7 3.3 copy-start.3
  86.7 1.9 copy-start.5
  87.1 3.0 copy-start.19
  90.1 15.0 %slice-start = ((s8[4718592]{0:T(1024)(128)(4,1)}), s8[4194304]{0:T(1024)(128)(4,1)S(1)}, s32[]{:S(2)}) async-start(s8[4718592]{0:T(1024)(128)(4,1)} %bitcast.81), calls=%async_computation.19 | async-start | bytes 8388608
  93.5 11.7 copy-start.14
  93.5 11.7 copy-start.10
  93.5 11.7 slice-start.1
  105.1 3.9 copy-start.29
  109.6 1.3 copy-start.6
  133.9 1.9 copy-start.2
  142.4 2.6 copy-start.4
  145.0 200.0 %reduce-scatter.21.cloned.1.call-start = ((), (), s32[]{:S(2)}) async-start(), calls=%async_computation.17 | async-start | bytes 1216512 | tf_op jit(solution)/shard_map/reduce_scatter | solution.py:218
  155.1 2.6 copy-start.12
  157.7 287.8 %reduce-scatter.23.cloned.1.call-start = ((), (), s32[]{:S(2)}) async-start(), calls=%async_computation.18 | async-start | bytes 1216512 | tf_op jit(solution)/shard_map/reduce_scatter | solution.py:218
  170.1 2.6 copy-start.7
  172.7 373.6 %reduce-scatter.13.cloned.1.call-start = ((), (), s32[]{:S(2)}) async-start(), calls=%async_computation.9 | async-start | bytes 1216512 | tf_op jit(solution)/shard_map/reduce_scatter | solution.py:218
  176.1 482.1 %reduce-scatter.15.cloned.1.call-start = ((), (), s32[]{:S(2)}) async-start(), calls=%async_computation.11 | async-start | bytes 4866048 | tf_op jit(solution)/shard_map/reduce_scatter | solution.py:218
  185.2 585.9 %reduce-scatter.17.cloned.1.call-start = ((), (), s32[]{:S(2)}) async-start(), calls=%async_computation.13 | async-start | bytes 4866048 | tf_op jit(solution)/shard_map/reduce_scatter | solution.py:218
  194.1 633.7 %all-gather.21.cloned.1.call-start = ((), (), s32[]{:S(2)}) async-start(), calls=%async_computation.15 | async-start | bytes 1216512 | tf_op jit(solution)/shard_map/all_gather | solution.py:12
  194.4 0.6 copy-start.17
  195.1 688.6 %all-gather.9.cloned.1.call-start = ((), (), s32[]{:S(2)}) async-start(), calls=%async_computation.6 | async-start | bytes 1216512 | tf_op jit(solution)/shard_map/all_gather | solution.py:221
  244.1 695.6 %all-gather.11.cloned.1.call-start = ((), (), s32[]{:S(2)}) async-start(), calls=%async_computation.7 | async-start | bytes 1216512 | tf_op jit(solution)/shard_map/all_gather | solution.py:221
  345.0 650.4 %all-gather.13.cloned.1.call-start = ((), (), s32[]{:S(2)}) async-start(), calls=%async_computation.8 | async-start | bytes 1216512 | tf_op jit(solution)/shard_map/all_gather | solution.py:221
  445.5 605.8 %all-gather.15.cloned.1.call-start = ((), (), s32[]{:S(2)}) async-start(), calls=%async_computation.10 | async-start | bytes 1216512 | tf_op jit(solution)/shard_map/all_gather | solution.py:221
  546.3 570.4 %all-gather.17.cloned.1.call-start = ((), (), s32[]{:S(2)}) async-start(), calls=%async_computation.12 | async-start | bytes 4866048 | tf_op jit(solution)/shard_map/all_gather | solution.py:221
  658.2 523.8 %all-gather.19.cloned.1.call-start = ((), (), s32[]{:S(2)}) async-start(), calls=%async_computation.14 | async-start | bytes 4866048 | tf_op jit(solution)/shard_map/all_gather | solution.py:221
  771.2 2.7 copy-start.16
  771.2 2.7 copy-start.22
  773.9 1.2 copy-start.13
  773.9 1.6 copy-start.15
Sparse Core Ops, SparseCore 0:
  145.1 98.8 reduce-scatter.18
  249.7 95.2 reduce-scatter.20
  350.1 95.2 reduce-scatter.22
  450.9 95.2 reduce-scatter.12
  552.2 105.9 reduce-scatter.14
  665.0 106.1 reduce-scatter.16
  774.6 53.1 all-gather.20
  830.7 52.9 all-gather.8
  886.6 52.9 all-gather.10
  942.4 52.9 all-gather.12
  998.3 52.9 all-gather.14
  1054.0 62.5 all-gather.16
  1119.5 62.4 all-gather.18
